TPU v7x, 32 devices: a whole 2x2x4 slice. The times are simulated.
32 devices in a mesh: samp: 16 (over z, y, x), feat: 2 (over core).
Axes of the slice: x: 2, y: 2, z: 4, core: 2. Of those that a mesh axis runs over, the one named last changes fastest.
Arguments:
- design_matrix: bfloat16 [2048, 32768], P('samp', 'feat'), may hold values from -0.046875 to 0.046875
- labels: int32 [2048], P('samp'), may hold values from 0 to 1
- weights: float32 [16, 32768], P(None, ('feat', 'samp')), may hold values from -6 to 6
- lambdas: float32 [16], replicated, may hold values from 0.05 to 1
- sketch: bfloat16 [32768, 384], P(('feat', 'samp')), may hold values from -0.03125 to 0.03125
- sketch_values: float32 [384], replicated, may hold values from 0.05 to 2
Outputs:
- new_weights: float32 [16, 32768], P(None, ('feat', 'samp'))
All inputs are finite; a program needn't handle non-finite values.
Results may differ from a plain program's by a relative error of at most 0.004.
Values may be sent and summed in bfloat16 or wider, within the bound.
No kernel may reach another device: no remote copies, remote signals or barrier semaphores. Data moves between devices by JAX's collectives and lax.ppermute only.
A program may use at most 64 MiB of HBM per device.

v0:
```python
import jax
import jax.numpy as jnp
from jax import lax
from jax.sharding import PartitionSpec as P

ITERS = 2


def shards(design_matrix, labels, weights, lambdas, sketch, sketch_values):
    sketch_full = sketch.astype(jnp.float32)
    smallest = jnp.min(sketch_values)
    ratios = (smallest + lambdas[:, None]) / (sketch_values[None, :] + lambdas[:, None]) - 1.0

    def apply_rows(vector):
        vector_half = vector.astype(jnp.bfloat16)
        partial_rows = lax.dot_general(
            lax.all_gather(vector_half, "samp", axis=1, tiled=True),
            design_matrix,
            (((1,), (1,)), ((), ())),
            preferred_element_type=jnp.float32,
        )
        return lax.psum(partial_rows, "feat")

    def apply_columns(values):
        return lax.psum_scatter(
            lax.dot_general(
                design_matrix, values, (((0,), (1,)), ((), ())), preferred_element_type=jnp.float32
            ),
            "samp",
            scatter_dimension=0,
            tiled=True,
        ).T

    def precondition(residual):
        projected = jnp.dot(residual, sketch_full, precision=lax.Precision.HIGHEST)
        projected = lax.psum(projected, ("samp", "feat"))
        correction = lax.dot_general(
            ratios * projected,
            sketch_full,
            (((1,), (1,)), ((), ())),
            precision=lax.Precision.HIGHEST,
        )
        precond_res = residual + correction
        res_dot = lax.psum(jnp.sum(residual * precond_res, axis=1), ("samp", "feat"))
        return (precond_res, res_dot)

    logits = apply_rows(weights)
    probability = jax.nn.sigmoid(logits)
    hessian_diag = probability * (1.0 - probability)
    miss_rows = (probability - labels[None, :].astype(jnp.float32)).astype(jnp.bfloat16)
    gradient = apply_columns(miss_rows) + lambdas[:, None] * weights
    residual = -gradient
    precond_res, res_dot = precondition(residual)
    direction = precond_res
    update = jnp.zeros_like(residual)
    for iteration in range(ITERS):
        image_rows = apply_rows(direction)
        hess_dir = (
            apply_columns((hessian_diag * image_rows).astype(jnp.bfloat16))
            + lambdas[:, None] * direction
        )
        curvature = lax.psum(jnp.sum(direction * hess_dir, axis=1), ("samp", "feat"))
        step_size = res_dot / curvature
        update = update + step_size[:, None] * direction
        if iteration + 1 < ITERS:
            residual = residual - step_size[:, None] * hess_dir
            precond_res, new_dot = precondition(residual)
            direction = precond_res + (new_dot / res_dot)[:, None] * direction
            res_dot = new_dot
    return weights + update


def solution(mesh):
    return jax.shard_map(
        shards,
        mesh=mesh,
        in_specs=(
            P("samp", "feat"),
            P("samp"),
            P(None, ("feat", "samp")),
            P(),
            P(("feat", "samp"), None),
            P(),
        ),
        out_specs=P(None, ("feat", "samp")),
        check_vma=False,
    )
```

profile of v0, /device:TPU:10, one launch (start us, length us, event | category | flops | bytes accessed | tf_op | source)
XLA Modules:
  0.0 596.1 jit_solution(18189731865618623638)
XLA Ops:
  8.1 33.0 %all_gather.9 = bf16[16,16384]{1,0:T(8,128)(2,1)S(1)} all-gather(bf16[16,1024]{1,0:T(8,128)(2,1)S(1)} %convert_element_type.23), channel_id=1, replica_groups=mesh['samp'=16,'feat'=2] {'samp'}, dimensions={1}, use_global_device_ids=true | all-gather | bytes 557056 | tf_op jit(solution)/shard_map/all_gather | solution.py:17
  41.1 3.4 fusion.22
  44.5 2.6 psum.63
  47.1 3.8 convolution_bitcast_fusion.2
  52.3 73.3 %reduce-scatter.4.cloned.1.call-done = f32[1024,16]{0,1:T(8,128)} async-done(((f32[16384,16]{0,1:T(8,128)}), f32[1024,16]{0,1:T(8,128)}) %reduce-scatter.4.cloned.1.call-update) | async-done | bytes 65552 | tf_op jit(solution)/shard_map/reduce_scatter | solution.py:25
  125.6 0.9 fusion.2
  127.0 50.1 %psum.64 = f32[16,384]{1,0:T(8,128)S(1)} all-reduce(f32[16,384]{1,0:T(8,128)S(1)} %fusion.23), channel_id=1, replica_groups=mesh['samp'=16,'feat'=2] {'samp','feat'}, use_global_device_ids=true, to_apply=%region_3.0 | all-reduce | flops 6144 | bytes 49152 | tf_op jit(solution)/shard_map/psum | solution.py:36
  177.8 32.0 %all_gather.10 = bf16[16,16384]{1,0:T(8,128)(2,1)S(1)} all-gather(bf16[16,1024]{1,0:T(8,128)(2,1)S(1)} %get-tuple-element.9), channel_id=1, replica_groups=mesh['samp'=16,'feat'=2] {'samp'}, dimensions={1}, use_global_device_ids=true | all-gather | bytes 557056 | tf_op jit(solution)/shard_map/all_gather | solution.py:17
  209.8 3.4 fusion.24
  213.1 2.5 psum.66
  215.6 3.8 convolution_bitcast_fusion.1
  219.5 71.6 %reduce-scatter.6.cloned.1.call-done = f32[1024,16]{0,1:T(8,128)} async-done(((f32[16384,16]{0,1:T(8,128)}), f32[1024,16]{0,1:T(8,128)}) %reduce-scatter.6.cloned.1.call-update) | async-done | bytes 65552 | tf_op jit(solution)/shard_map/reduce_scatter | solution.py:25
  291.1 1.0 multiply_reduce_fusion.1
  292.1 49.7 %all-reduce = (f32[16]{0:T(128)S(1)}, f32[16]{0:T(128)S(1)}) all-reduce(f32[16]{0:T(128)S(1)} %get-tuple-element.6, f32[16]{0:T(128)S(1)} %get-tuple-element.5), channel_id=1, replica_groups=mesh['samp'=16,'feat'=2] {'samp','feat'}, use_global_device_ids=true, to_apply=%region_5.0 | all-reduce | flops 32 | bytes 256 | tf_op jit(solution)/shard_map/psum | solution.py:44
  341.9 0.9 multiply_subtract_fusion
  343.2 38.3 %psum.68 = f32[16,384]{1,0:T(8,128)S(1)} all-reduce(f32[16,384]{1,0:T(8,128)S(1)} %fusion.25), channel_id=1, replica_groups=mesh['samp'=16,'feat'=2] {'samp','feat'}, use_global_device_ids=true, to_apply=%region_10.0 | all-reduce | flops 6144 | bytes 49152 | tf_op jit(solution)/shard_map/psum | solution.py:36
  382.3 41.9 %psum.69 = f32[16]{0:T(128)S(1)} all-reduce(f32[16]{0:T(128)S(1)} %get-tuple-element.11), channel_id=1, replica_groups=mesh['samp'=16,'feat'=2] {'samp','feat'}, use_global_device_ids=true, to_apply=%region_12.0 | all-reduce | flops 16 | bytes 128 | tf_op jit(solution)/shard_map/psum | solution.py:44
  424.3 31.8 %all_gather.11 = bf16[16,16384]{1,0:T(8,128)(2,1)S(1)} all-gather(bf16[16,1024]{1,0:T(8,128)(2,1)S(1)} %fusion.20), channel_id=1, replica_groups=mesh['samp'=16,'feat'=2] {'samp'}, dimensions={1}, use_global_device_ids=true | all-gather | bytes 557056 | tf_op jit(solution)/shard_map/all_gather | solution.py:17
  456.1 3.4 fusion.26
  459.5 2.5 psum.70
  462.0 3.9 convolution_bitcast_fusion
  465.8 72.2 %reduce-scatter.8.cloned.1.call-done = f32[1024,16]{0,1:T(8,128)} async-done(((f32[16384,16]{0,1:T(8,128)}), f32[1024,16]{0,1:T(8,128)}) %reduce-scatter.8.cloned.1.call-update) | async-done | bytes 65552 | tf_op jit(solution)/shard_map/reduce_scatter | solution.py:25
  538.1 1.0 fusion.1
  539.1 49.8 %psum.71 = f32[16]{0:T(128)S(1)} all-reduce(f32[16]{0:T(128)S(1)} %fusion.1), channel_id=1, replica_groups=mesh['samp'=16,'feat'=2] {'samp','feat'}, use_global_device_ids=true, to_apply=%region_16.0 | all-reduce | flops 16 | bytes 128 | tf_op jit(solution)/shard_map/psum | solution.py:62
  (27 shorter events, 6.2 us)
Async XLA Ops:
  6.5 120.0 %copy-start = (bf16[1024,384]{1,0:T(8,128)(2,1)S(1)}, bf16[1024,384]{1,0:T(8,128)(2,1)}, u32[]{:S(2)}) copy-start(bf16[1024,384]{1,0:T(8,128)(2,1)} %param.10) | copy-start | bytes 2359300
  6.5 119.1 %reduce-scatter.4.cloned.1.call-start = ((), (), s32[]{:S(2)}) async-start(), calls=%async_computation.3 | async-start | bytes 1114112 | tf_op jit(solution)/shard_map/reduce_scatter | solution.py:25
  44.4 6.6 %copy-start.3 = (f32[384]{0:T(512)S(1)}, f32[384]{0:T(512)}, u32[]{:S(2)}) copy-start(f32[384]{0:T(512)} %param.11) | copy-start | bytes 4612
  44.4 7.2 %copy-start.2 = (f32[16]{0:T(128)S(1)}, f32[16]{0:T(128)}, u32[]{:S(2)}) copy-start(f32[16]{0:T(128)} %param.9) | copy-start | bytes 196
  44.4 81.2 %copy-start.1 = (f32[16,1024]{1,0:T(8,128)S(1)}, f32[16,1024]{1,0:T(8,128)}, u32[]{:S(2)}) copy-start(f32[16,1024]{1,0:T(8,128)} %param.8) | copy-start | bytes 196612
  51.0 240.1 %reduce-scatter.6.cloned.1.call-start = ((), (), s32[]{:S(2)}) async-start(), calls=%async_computation.4 | async-start | bytes 1114112 | tf_op jit(solution)/shard_map/reduce_scatter | solution.py:25
  219.5 318.6 %reduce-scatter.8.cloned.1.call-start = ((), (), s32[]{:S(2)}) async-start(), calls=%async_computation.5 | async-start | bytes 1114112 | tf_op jit(solution)/shard_map/reduce_scatter | solution.py:25
Sparse Core Ops, SparseCore 0:
  51.1 74.4 reduce-scatter.3
  219.6 71.4 reduce-scatter.5
  466.0 72.0 reduce-scatter.7
where the time goes:
time: 597 us; the launch traced here: 596 us
  blocking collectives  334 us (56%)
  waiting for transfers between devices  217 us (36%)
  matrix products  24.1 us (4%)
  between operations  13.2 us (2%)
  other arithmetic  7.54 us (1%)
    reduce_scatter x3, waiting for transfers between devices, apply_columns(): lax.psum_scatter(lax.dot_general(design_matrix, values, (((0,), (1,)), ((...  217 us
    all_gather x3, blocking collectives, apply_rows(): lax.all_gather(vector_half, 'samp', axis=1, tiled=True)  96.7 us
    psum x2, blocking collectives, precondition(): lax.psum(jnp.sum(residual * precond_res, axis=1), ('samp', 'feat'))  91.6 us
    psum x2, blocking collectives, precondition(): projected = lax.psum(projected, ('samp', 'feat'))  88.3 us
    psum x1, blocking collectives, shards(): lax.psum(jnp.sum(direction * hess_dir, axis=1), ('samp', 'feat'))  49.8 us
  transfers between devices with their start and end apart: 3, of which 3 were waited for; matrix products, arithmetic and copies ran while one was open for 0% of the time, Pallas kernels for 0%

commit v1 on v0

--- a/solution.py
+++ b/solution.py
@@ -14,7 +14,10 @@
     def apply_rows(vector):
         vector_half = vector.astype(jnp.bfloat16)
         partial_rows = lax.dot_general(
-            lax.all_gather(vector_half, "samp", axis=1, tiled=True),
+            jnp.concatenate(
+                lax.all_to_all(jnp.stack([vector_half] * lax.axis_size("samp")), "samp", 0, 0),
+                axis=1,
+            ),
             design_matrix,
             (((1,), (1,)), ((), ())),
             preferred_element_type=jnp.float32,

time: 597 us -> 539 us (0.903)
  blocking collectives: 334 us -> 271 us
  starting transfers between devices: 0.09 us -> 7.32 us
    all_gather x3 -> x0, blocking collectives: 96.7 us -> none  [apply_rows(): lax.all_gather(vector_half, 'samp', axis=1, tiled=True)]
    all_to_all x0 -> x2, blocking collectives: none -> 33.9 us  [apply_rows(): lax.all_to_all(jnp.stack([vector_half] * lax.axis_size('samp')), 'samp',...]
    reduce_scatter x3, waiting for transfers between devices: 217 us -> 201 us  [apply_columns(): lax.psum_scatter(lax.dot_general(design_matrix, values, (((0,), (1,)), ((...]
    all_to_all x0 -> x1, waiting for transfers between devices: none -> 12.9 us  [apply_rows(): lax.all_to_all(jnp.stack([vector_half] * lax.axis_size('samp')), 'samp',...]
    all_to_all x0 -> x1, starting transfers between devices: none -> 7.2 us  [apply_rows(): lax.all_to_all(jnp.stack([vector_half] * lax.axis_size('samp')), 'samp',...]
  transfers between devices with their start and end apart: 3 -> 4, of which waited for: 3 -> 4; matrix products, arithmetic and copies ran while one was open for 0% -> 0% of each run, Pallas kernels for 0% -> 0%
where the time goes in v1:
time: 539 us; the launch traced here: 538 us
  blocking collectives  271 us (50%)
  waiting for transfers between devices  214 us (40%)
  matrix products  24.1 us (4%)
  between operations  13.2 us (2%)
  other arithmetic  7.54 us (1%)
  starting transfers between devices  7.32 us (1%)
    reduce_scatter x3, waiting for transfers between devices, apply_columns(): lax.psum_scatter(lax.dot_general(design_matrix, values, (((0,), (1,)), ((...  201 us
    psum x2, blocking collectives, precondition(): lax.psum(jnp.sum(residual * precond_res, axis=1), ('samp', 'feat'))  91.6 us
    psum x2, blocking collectives, precondition(): projected = lax.psum(projected, ('samp', 'feat'))  88.2 us
    psum x1, blocking collectives, shards(): lax.psum(jnp.sum(direction * hess_dir, axis=1), ('samp', 'feat'))  50 us
    all_to_all x2, blocking collectives, apply_rows(): lax.all_to_all(jnp.stack([vector_half] * lax.axis_size('samp')), 'samp',...  33.9 us
    all_to_all x1, waiting for transfers between devices, apply_rows(): lax.all_to_all(jnp.stack([vector_half] * lax.axis_size('samp')), 'samp',...  12.9 us
    dot_general x3, matrix products, apply_columns(): lax.dot_general(design_matrix, values, (((0,), (1,)), ((), ())), preferre...  11.5 us
  transfers between devices with their start and end apart: 4, of which 4 were waited for; matrix products, arithmetic and copies ran while one was open for 0% of the time, Pallas kernels for 0%

profile of v1, /device:TPU:10, one launch (start us, length us, event | category | flops | bytes accessed | tf_op | source)
XLA Modules:
  0.0 538.2 jit_solution(7470127569740504813)
XLA Ops:
  8.3 7.2 %all-to-all-start = ((bf16[16,16,1024]{2,1,0:T(8,128)(2,1)}), bf16[16,16,1024]{2,1,0:T(8,128)(2,1)S(1)}, u32[]{:S(2)}, u32[]{:S(2)}) async-start(bf16[16,16,1024]{2,1,0:T(8,128)(2,1)} %stack.6), calls=%async_computation | async-start | bytes 1048576 | tf_op jit(solution)/shard_map/all_to_all | solution.py:18
  16.2 12.9 %all-to-all-done = bf16[16,16,1024]{2,1,0:T(8,128)(2,1)S(1)} async-done(((bf16[16,16,1024]{2,1,0:T(8,128)(2,1)}), bf16[16,16,1024]{2,1,0:T(8,128)(2,1)S(1)}, u32[]{:S(2)}, u32[]{:S(2)}) %all-to-all-start) | async-done | bytes 524320 | tf_op jit(solution)/shard_map/all_to_all | solution.py:18
  29.1 3.4 fusion.22
  32.5 2.6 psum.63
  35.1 3.8 convolution_bitcast_fusion.2
  40.3 66.1 %reduce-scatter.4.cloned.1.call-done = f32[1024,16]{0,1:T(8,128)} async-done(((f32[16384,16]{0,1:T(8,128)}), f32[1024,16]{0,1:T(8,128)}) %reduce-scatter.4.cloned.1.call-update) | async-done | bytes 65552 | tf_op jit(solution)/shard_map/reduce_scatter | solution.py:28
  107.8 50.0 %psum.64 = f32[16,384]{1,0:T(8,128)S(1)} all-reduce(f32[16,384]{1,0:T(8,128)S(1)} %fusion.23), channel_id=1, replica_groups=mesh['samp'=16,'feat'=2] {'samp','feat'}, use_global_device_ids=true, to_apply=%region_3.0 | all-reduce | flops 6144 | bytes 49152 | tf_op jit(solution)/shard_map/psum | solution.py:39
  158.6 17.0 %all_to_all.15 = bf16[16,16,1024]{2,1,0:T(8,128)(2,1)S(1)} all-to-all(bf16[16,16,1024]{2,1,0:T(8,128)(2,1)S(1)} %stack.7), channel_id=1, replica_groups=mesh['samp'=16,'feat'=2] {'samp'}, dimensions={0} | all-to-all | bytes 1048576 | tf_op jit(solution)/shard_map/all_to_all | solution.py:18
  175.6 3.4 fusion.24
  179.0 2.5 psum.66
  181.5 3.8 convolution_bitcast_fusion.1
  185.4 67.4 %reduce-scatter.6.cloned.1.call-done = f32[1024,16]{0,1:T(8,128)} async-done(((f32[16384,16]{0,1:T(8,128)}), f32[1024,16]{0,1:T(8,128)}) %reduce-scatter.6.cloned.1.call-update) | async-done | bytes 65552 | tf_op jit(solution)/shard_map/reduce_scatter | solution.py:28
  252.8 1.0 multiply_reduce_fusion.1
  253.8 49.7 %all-reduce = (f32[16]{0:T(128)S(1)}, f32[16]{0:T(128)S(1)}) all-reduce(f32[16]{0:T(128)S(1)} %get-tuple-element.6, f32[16]{0:T(128)S(1)} %get-tuple-element.5), channel_id=1, replica_groups=mesh['samp'=16,'feat'=2] {'samp','feat'}, use_global_device_ids=true, to_apply=%region_5.0 | all-reduce | flops 32 | bytes 256 | tf_op jit(solution)/shard_map/psum | solution.py:47
  303.5 0.9 multiply_subtract_fusion
  304.9 38.3 %psum.68 = f32[16,384]{1,0:T(8,128)S(1)} all-reduce(f32[16,384]{1,0:T(8,128)S(1)} %fusion.25), channel_id=1, replica_groups=mesh['samp'=16,'feat'=2] {'samp','feat'}, use_global_device_ids=true, to_apply=%region_10.0 | all-reduce | flops 6144 | bytes 49152 | tf_op jit(solution)/shard_map/psum | solution.py:39
  344.0 41.9 %psum.69 = f32[16]{0:T(128)S(1)} all-reduce(f32[16]{0:T(128)S(1)} %get-tuple-element.11), channel_id=1, replica_groups=mesh['samp'=16,'feat'=2] {'samp','feat'}, use_global_device_ids=true, to_apply=%region_12.0 | all-reduce | flops 16 | bytes 128 | tf_op jit(solution)/shard_map/psum | solution.py:47
  386.0 16.9 %all_to_all.16 = bf16[16,16,1024]{2,1,0:T(8,128)(2,1)S(1)} all-to-all(bf16[16,16,1024]{2,1,0:T(8,128)(2,1)S(1)} %stack.8), channel_id=1, replica_groups=mesh['samp'=16,'feat'=2] {'samp'}, dimensions={0} | all-to-all | bytes 1048576 | tf_op jit(solution)/shard_map/all_to_all | solution.py:18
  403.0 3.4 fusion.26
  406.3 2.5 psum.70
  408.8 3.9 convolution_bitcast_fusion
  412.7 67.3 %reduce-scatter.8.cloned.1.call-done = f32[1024,16]{0,1:T(8,128)} async-done(((f32[16384,16]{0,1:T(8,128)}), f32[1024,16]{0,1:T(8,128)}) %reduce-scatter.8.cloned.1.call-update) | async-done | bytes 65552 | tf_op jit(solution)/shard_map/reduce_scatter | solution.py:28
  480.0 1.0 fusion.1
  481.0 50.0 %psum.71 = f32[16]{0:T(128)S(1)} all-reduce(f32[16]{0:T(128)S(1)} %fusion.1), channel_id=1, replica_groups=mesh['samp'=16,'feat'=2] {'samp','feat'}, use_global_device_ids=true, to_apply=%region_16.0 | all-reduce | flops 16 | bytes 128 | tf_op jit(solution)/shard_map/psum | solution.py:65
  (34 shorter events, 8.2 us)
Async XLA Ops:
  6.5 100.9 %copy-start = (bf16[1024,384]{1,0:T(8,128)(2,1)S(1)}, bf16[1024,384]{1,0:T(8,128)(2,1)}, u32[]{:S(2)}) copy-start(bf16[1024,384]{1,0:T(8,128)(2,1)} %param.10) | copy-start | bytes 2359300
  8.3 20.8 %all-to-all-start = ((bf16[16,16,1024]{2,1,0:T(8,128)(2,1)}), bf16[16,16,1024]{2,1,0:T(8,128)(2,1)S(1)}, u32[]{:S(2)}, u32[]{:S(2)}) async-start(bf16[16,16,1024]{2,1,0:T(8,128)(2,1)} %stack.6), calls=%async_computation | async-start | bytes 1048576 | tf_op jit(solution)/shard_map/all_to_all | solution.py:18
  15.5 91.0 %reduce-scatter.4.cloned.1.call-start = ((), (), s32[]{:S(2)}) async-start(), calls=%async_computation.6 | async-start | bytes 1114112 | tf_op jit(solution)/shard_map/reduce_scatter | solution.py:28
  32.5 6.6 %copy-start.3 = (f32[384]{0:T(512)S(1)}, f32[384]{0:T(512)}, u32[]{:S(2)}) copy-start(f32[384]{0:T(512)} %param.11) | copy-start | bytes 4612
  32.5 7.2 %copy-start.2 = (f32[16]{0:T(128)S(1)}, f32[16]{0:T(128)}, u32[]{:S(2)}) copy-start(f32[16]{0:T(128)} %param.9) | copy-start | bytes 196
  32.5 74.0 %copy-start.1 = (f32[16,1024]{1,0:T(8,128)S(1)}, f32[16,1024]{1,0:T(8,128)}, u32[]{:S(2)}) copy-start(f32[16,1024]{1,0:T(8,128)} %param.8) | copy-start | bytes 196612
  39.0 213.8 %reduce-scatter.6.cloned.1.call-start = ((), (), s32[]{:S(2)}) async-start(), calls=%async_computation.7 | async-start | bytes 1114112 | tf_op jit(solution)/shard_map/reduce_scatter | solution.py:28
  185.3 294.6 %reduce-scatter.8.cloned.1.call-start = ((), (), s32[]{:S(2)}) async-start(), calls=%async_computation.8 | async-start | bytes 1114112 | tf_op jit(solution)/shard_map/reduce_scatter | solution.py:28
Sparse Core Ops, SparseCore 0:
  39.1 67.2 reduce-scatter.3
  185.5 67.3 reduce-scatter.5
  412.8 67.1 reduce-scatter.7
